TPU v7x, 32 devices: a whole 2x2x4 slice. The times are simulated.
32 devices in a mesh: section: 8 (over y, x, core), tp: 4 (over z).
Axes of the slice: x: 2, y: 2, z: 4, core: 2. Of those that a mesh axis runs over, the one named last changes fastest.
Arguments:
- stash: bfloat16 [8, 2, 256, 4096], P('section', None, 'tp'), may hold values from -660 to 660
- slot: int32 [8], P('section'), may hold values from 0 to 1
- doc_ids: int32 [8, 2, 256], P('section', None, 'tp'), may hold values from 0 to 3, never falling along the last dimension, each value on 1 to 128 neighbouring positions
- norm_gain: bfloat16 [4096], replicated, may hold values from 0.099609375 to 1.8984375
- w_query: bfloat16 [4096, 4096], P(None, 'tp'), may hold values from -21 to 21
- w_key: bfloat16 [4096, 1024], P(None, 'tp'), may hold values from -21 to 21
- value_weight: bfloat16 [4096, 1024], P(None, 'tp'), may hold values from -0.09375 to 0.09375
Outputs:
- received: bfloat16 [8, 256, 4096], P('section', None, 'tp')
Inputs may be any that keep to these rules, and one draw needn't show every extreme that they name: `doc_ids`: document numbers never fall along a micro-batch.
All inputs are finite; a program needn't handle non-finite values.
Results may differ from a plain program's by a relative error of at most 0.025.
The roundings to bfloat16 on the way count: a program that leaves them out, or rounds other values in their place, can miss the bound.
Values may be sent and summed in bfloat16 or wider, within the bound.
A program may use at most 64 MiB of HBM per device.

v0:
```python
import math
import jax
import jax.numpy as jnp
from jax import lax
from jax.sharding import PartitionSpec as P

HEAD_SIZE = 128
ROPE_BASE = 500000.0
NORM_EPSILON = 1e-05


def from_behind(block, axis, distance):
    devices = range(lax.axis_size(axis))
    route = [(i - distance, i) for i in devices if i - distance in devices]
    return lax.ppermute(block, axis, route)


def rotate(values, positions):
    head_width = values.shape[-1]
    half_width = head_width // 2
    freq_index = jnp.arange(half_width, dtype=jnp.float32)
    inverse = jnp.power(jnp.float32(ROPE_BASE), -2.0 * freq_index / head_width)
    angles = positions.astype(jnp.float32)[:, None] * inverse[None, :]
    cosine = jnp.concatenate([jnp.cos(angles), jnp.cos(angles)], -1)[:, None, :]
    sine_part = jnp.concatenate([jnp.sin(angles), jnp.sin(angles)], -1)[:, None, :]
    turned = jnp.concatenate([-values[..., half_width:], values[..., :half_width]], -1)
    return values * cosine + turned * sine_part


def normalize(stash_rows, norm_gain):
    widened = stash_rows.astype(jnp.float32)
    mean_square = jnp.mean(widened * widened, axis=-1, keepdims=True)
    return (widened * lax.rsqrt(mean_square + NORM_EPSILON) * norm_gain.astype(jnp.float32)).astype(
        jnp.bfloat16
    )


def project(normed, weight, positions, use_rope):
    length = normed.shape[0]
    product = jnp.dot(normed, weight, preferred_element_type=jnp.float32)
    if use_rope:
        product = rotate(product.reshape(length, -1, HEAD_SIZE), positions).reshape(length, -1)
    return product.astype(jnp.bfloat16)


def attend(queries, keys, values, doc_rows):
    length = queries.shape[0]
    kv_count = keys.shape[1] // HEAD_SIZE
    group_size = queries.shape[1] // HEAD_SIZE // kv_count
    grouped = queries.reshape(length, kv_count, group_size, HEAD_SIZE)
    key_heads = keys.reshape(length, kv_count, HEAD_SIZE)
    value_heads = values.reshape(length, kv_count, HEAD_SIZE)
    scores = jnp.einsum(
        "ihgd,jhd->hgij", grouped, key_heads, preferred_element_type=jnp.float32
    ) * (1.0 / math.sqrt(HEAD_SIZE))
    row_index = jnp.arange(length, dtype=jnp.int32)[:, None]
    col_index = jnp.arange(length, dtype=jnp.int32)[None, :]
    allowed = (col_index <= row_index) & (doc_rows[None, :] == doc_rows[:, None])
    scores = jnp.where(allowed, scores, -1e30)
    row_max = jnp.max(scores, axis=-1, keepdims=True)
    score_exponent = jnp.exp(scores - row_max)
    softmax_weights = (score_exponent / jnp.sum(score_exponent, axis=-1, keepdims=True)).astype(
        jnp.bfloat16
    )
    context = jnp.einsum(
        "hgij,jhd->ihgd", softmax_weights, value_heads, preferred_element_type=jnp.float32
    )
    return context.reshape(length, -1).astype(jnp.bfloat16)


def per_device(stash, slot, doc_ids, norm_gain, w_query, w_key, value_weight):
    group_count = lax.axis_size("tp")
    local_length = stash.shape[2]
    total_length = local_length * group_count
    chosen_slot = slot[0]
    picked = lax.dynamic_index_in_dim(stash[0], chosen_slot, 0, keepdims=False)
    doc_rows = lax.dynamic_index_in_dim(doc_ids[0], chosen_slot, 0, keepdims=False)
    doc_all = jnp.zeros((total_length,), jnp.int32)
    piece_rows = lax.all_gather(picked, "tp", axis=0, tiled=True)
    piece_docs = lax.all_gather(doc_rows, "tp", axis=0, tiled=True)
    piece_count = piece_rows.shape[0]
    positions = jnp.arange(piece_count, dtype=jnp.int32)
    normed = normalize(piece_rows, norm_gain)
    queries = project(normed, w_query, positions, True)
    keys = project(normed, w_key, positions, True)
    values = project(normed, value_weight, positions, False)
    doc_all = lax.dynamic_update_slice_in_dim(doc_all, piece_docs, jnp.int32(0), 0)
    queries, keys, values, doc_all = (queries, keys, values, doc_all)
    context = attend(queries, keys, values, doc_all)
    return from_behind(context[None], "section", 1)


def solution(mesh):
    placed = (
        P("section", None, "tp", None),
        P("section"),
        P("section", None, "tp"),
        P(),
        P(None, "tp"),
        P(None, "tp"),
        P(None, "tp"),
    )
    return jax.shard_map(
        per_device, mesh=mesh, in_specs=placed, out_specs=P("section", None, "tp"), check_vma=False
    )
```

profile of v0, /device:TPU:4, one launch (start us, length us, event | category | flops | bytes accessed | tf_op | source)
XLA Modules:
  0.0 92.8 jit_solution(12643340829580763346)
XLA Ops:
  6.5 0.0 copy-start
  6.5 0.0 copy-start.3
  6.5 0.0 copy-start.2
  6.5 0.0 all-gather.4.cloned.1.call-start
  7.3 1.9 %constant_dynamic-slice_fusion = bf16[1,1,64,4096]{3,2,1,0:T(8,128)(2,1)} fusion(bf16[1,2,64,4096]{3,2,1,0:T(8,128)(2,1)} %param.7, s32[]{:T(128)S(6)} %select_n.10), kind=kLoop, calls=%fused_computation.37 | loop fusion | bytes 1048580 | tf_op jit(solution)/shard_map/jit(dynamic_index_in_dim)/dynamic_slice | solution.py:76
  9.2 0.0 all-gather.4.cloned.1.call-update
  9.3 0.7 convert_element_type.52
  10.0 0.3 multiply_cosine_fusion
  10.3 0.1 copy.9
  10.4 0.1 copy.8
  10.5 0.0 copy-done.3
  10.5 0.6 dynamic-slice.2
  11.6 0.0 copy-done.2
  11.7 0.1 bitcast_dynamic-update-slice_fusion
  11.8 8.4 %all-reduce = s32[256]{0:T(256)S(1)} all-reduce(s32[256]{0:T(256)S(1)} %bitcast_dynamic-update-slice_fusion), channel_id=3, replica_groups=mesh['section'=8,'tp'=4] {'tp'}, use_global_device_ids=true, to_apply=%add | all-reduce | flops 256 | bytes 2048 | tf_op jit(solution)/shard_map/all_gather | solution.py:80
  20.2 0.1 fusion.12
  20.3 35.9 %all-gather.4.cloned.1.call-done = bf16[1,1,256,4096]{3,2,1,0:T(8,128)(2,1)} async-done(((bf16[1,1,64,4096]{3,2,1,0:T(8,128)(2,1)}), bf16[1,1,256,4096]{3,2,1,0:T(8,128)(2,1)}) %all-gather.4.cloned.1.call-update) | async-done | bytes 2097168 | tf_op jit(solution)/shard_map/all_gather | solution.py:79
  56.3 0.0 copy-start.1
  56.3 2.2 %fusion.1 = f32[256]{0:T(256)S(1)} fusion(bf16[1,1,256,4096]{3,2,1,0:T(8,128)(2,1)} %all-gather.4.cloned.1.call-done), kind=kLoop, calls=%fused_computation.3 | loop fusion | flops 3145472 | bytes 2098176 | tf_op jit(solution)/shard_map/reduce_sum | solution.py:32
  58.5 0.0 copy-done
  58.5 0.0 copy-done.1
  58.5 1.1 %fusion.23 = f32[256,256]{0,1:T(8,128)S(1)} fusion(bf16[4096,256]{1,0:T(8,128)(2,1)S(1)} %copy-done, bf16[1,1,256,4096]{3,2,1,0:T(8,128)(2,1)S(1)} %copy-done.1, f32[4096]{0:T(1024)S(1)} %convert_element_type.52, f32[256]{0:T(256)S(1)} %add_rsqrt_fusion), kind=kOutput, calls=%fused_computation.41 | convolution fusion | flops 541065216 | bytes 4473856 | tf_op jit(solution)/shard_map/dot_general | solution.py:40
  59.8 5.7 %fusion.21 = f32[256,1024]{1,0:T(8,128)S(1)} fusion(bf16[4096,1024]{1,0:T(8,128)(2,1)} %param.11, bf16[1,1,256,4096]{3,2,1,0:T(8,128)(2,1)S(1)} %copy-done.1, f32[4096]{0:T(1024)S(1)} %convert_element_type.52, f32[256]{0:T(256)S(1)} %add_rsqrt_fusion), kind=kOutput, calls=%fused_computation.40 | convolution fusion | flops 2151677952 | bytes 11551744 | tf_op jit(solution)/shard_map/dot_general | solution.py:40
  65.5 0.2 copy.20
  65.7 0.3 slice_negate_fusion
  66.1 0.4 maximum_multiply_fusion
  66.4 0.1 mul.129
  66.5 0.6 fusion.5
  67.1 0.4 reshape.69
  67.5 2.2 %fusion.26 = (f32[2,4,256]{2,1,0:T(4,128)S(1)}, f32[2,4,256,256]{2,3,1,0:T(8,128)}) fusion(pred[256,256]{0,1:T(8,128)(4,1)S(1)} %fusion.12, bf16[256,2,128,1]{0,2,3,1:T(8,128)(2,1)S(1)} %bitcast.66, bf16[256,2,4,128]{3,2,1,0:T(4,128)(2,1)S(1)} %reshape.69), kind=kOutput, calls=%fused_computation.42 | convolution fusion | flops 136315136 | bytes 2826240 | tf_op jit(solution)/shard_map/sub | solution.py:61
  69.7 0.0 copy-start.4
  69.7 3.5 %convolution_convert_fusion.1 = bf16[256,256]{0,1:T(8,128)(2,1)S(1)} fusion(bf16[4096,256]{1,0:T(8,128)(2,1)} %param.13, bf16[1,1,256,4096]{3,2,1,0:T(8,128)(2,1)} %all-gather.4.cloned.1.call-done, f32[4096]{0:T(1024)S(1)} %convert_element_type.52, f32[256]{0:T(256)S(1)} %add_rsqrt_fusion), kind=kOutput, calls=%fused_computation.11 | convolution fusion | flops 541130752 | bytes 4342784 | tf_op jit(solution)/shard_map/dot_general | solution.py:40
  73.2 0.0 copy-done.4
  73.2 0.3 convolution_convert_fusion
  73.6 0.2 copy.13
  73.8 1.9 %collective-permute-start = (bf16[1,256,1024]{2,1,0:T(8,128)(2,1)S(1)}, bf16[1,256,1024]{2,1,0:T(8,128)(2,1)S(1)}, u32[]{:S(2)}, u32[]{:S(2)}) collective-permute-start(bf16[1,256,1024]{2,1,0:T(8,128)(2,1)S(1)} %copy.13), channel_id=1, source_target_pairs={{0,4},{4,8},{8,12},{12,16},{16,20},{20,24},{24,28},{1,5},{5,9},{9,... | collective-permute-start | bytes 1572872 | tf_op jit(solution)/shard_map/ppermute | solution.py:15
  75.7 9.5 %collective-permute-done = bf16[1,256,1024]{2,1,0:T(8,128)(2,1)S(1)} collective-permute-done((bf16[1,256,1024]{2,1,0:T(8,128)(2,1)S(1)}, bf16[1,256,1024]{2,1,0:T(8,128)(2,1)S(1)}, u32[]{:S(2)}, u32[]{:S(2)}) %collective-permute-start) | collective-permute-done | bytes 524320 | tf_op jit(solution)/shard_map/ppermute | solution.py:15
  85.2 0.8 copy.37
  (8 shorter events, 0.1 us)
Async XLA Ops:
  6.5 52.0 %copy-start = (bf16[4096,256]{1,0:T(8,128)(2,1)S(1)}, bf16[4096,256]{1,0:T(8,128)(2,1)}, u32[]{:S(2)}) copy-start(bf16[4096,256]{1,0:T(8,128)(2,1)} %param.12) | copy-start | bytes 6291460
  6.5 4.0 %copy-start.3 = (u32[32]{0:T(128)S(1)}, u32[32]{0:T(128)}, u32[]{:S(2)}) copy-start(u32[32]{0:T(128)} %constant.37) | copy-start | bytes 388
  6.5 5.1 %copy-start.2 = (s32[1,2,64]{2,1,0:T(2,128)S(1)}, s32[1,2,64]{2,1,0:T(2,128)}, u32[]{:S(2)}) copy-start(s32[1,2,64]{2,1,0:T(2,128)} %param.9) | copy-start | bytes 1540
  6.5 49.7 %all-gather.4.cloned.1.call-start = ((), (), s32[]{:S(2)}) async-start(), calls=%async_computation | async-start | bytes 2621440 | tf_op jit(solution)/shard_map/all_gather | solution.py:79
  56.3 2.3 %copy-start.1 = (bf16[1,1,256,4096]{3,2,1,0:T(8,128)(2,1)S(1)}, bf16[1,1,256,4096]{3,2,1,0:T(8,128)(2,1)}, u32[]{:S(2)}) copy-start(bf16[1,1,256,4096]{3,2,1,0:T(8,128)(2,1)} %all-gather.4.cloned.1.call-done) | copy-start | bytes 6291460
  69.7 3.5 %copy-start.4 = (f32[2,4,256,256]{2,3,1,0:T(8,128)S(1)}, f32[2,4,256,256]{2,3,1,0:T(8,128)}, u32[]{:S(2)}) copy-start(f32[2,4,256,256]{2,3,1,0:T(8,128)} %get-tuple-element.12) | copy-start | bytes 6291460
  73.8 11.4 %collective-permute-start = (bf16[1,256,1024]{2,1,0:T(8,128)(2,1)S(1)}, bf16[1,256,1024]{2,1,0:T(8,128)(2,1)S(1)}, u32[]{:S(2)}, u32[]{:S(2)}) collective-permute-start(bf16[1,256,1024]{2,1,0:T(8,128)(2,1)S(1)} %copy.13), channel_id=1, source_target_pairs={{0,4},{4,8},{8,12},{12,16},{16,20},{20,24},{24,28},{1,5},{5,9},{9,... | collective-permute-start | bytes 1572872 | tf_op jit(solution)/shard_map/ppermute | solution.py:15
Sparse Core Ops, SparseCore 0:
  9.4 46.8 all-gather.3
where the time goes:
time: 93.1 us; the launch traced here: 92.8 us
  waiting for transfers between devices  45.4 us (49%)
  between operations  15 us (16%)
  matrix products  12.9 us (14%)
  blocking collectives  8.44 us (9%)
  other arithmetic  4.79 us (5%)
  local copies, waits for them, and re-layouts  4.37 us (5%)
  starting transfers between devices  1.92 us (2%)
    all_gather x1, waiting for transfers between devices, per_device(): piece_rows = lax.all_gather(picked, 'tp', axis=0, tiled=True)  35.9 us
    dot_general x3, matrix products, project(): product = jnp.dot(normed, weight, preferred_element_type=jnp.float32)  10.4 us
    ppermute x1, waiting for transfers between devices, from_behind(): return lax.ppermute(block, axis, route)  9.47 us
    all_gather x1, blocking collectives, per_device(): piece_docs = lax.all_gather(doc_rows, 'tp', axis=0, tiled=True)  8.44 us
    reduce_sum x1, other arithmetic, normalize(): mean_square = jnp.mean(widened * widened, axis=-1, keepdims=True)  2.23 us
    sub x1, matrix products, attend(): score_exponent = jnp.exp(scores - row_max)  2.19 us
    ppermute x1, starting transfers between devices, from_behind(): return lax.ppermute(block, axis, route)  1.92 us
    dynamic_slice x1, local copies, waits for them, and re-layouts, per_device(): picked = lax.dynamic_index_in_dim(stash[0], chosen_slot, 0, keepdims=False)  1.87 us
  transfers between devices with their start and end apart: 2, of which 2 were waited for; matrix products, arithmetic and copies ran while one was open for 2% of the time, Pallas kernels for 0%

commit v1 on v0

--- a/solution.py
+++ b/solution.py
@@ -76,7 +76,12 @@
     picked = lax.dynamic_index_in_dim(stash[0], chosen_slot, 0, keepdims=False)
     doc_rows = lax.dynamic_index_in_dim(doc_ids[0], chosen_slot, 0, keepdims=False)
     doc_all = jnp.zeros((total_length,), jnp.int32)
-    piece_rows = lax.all_gather(picked, "tp", axis=0, tiled=True)
+    ring = [picked]
+    for hop in range(3):
+        ring.append(lax.ppermute(ring[-1], "tp", [(dev, (dev + 1) % 4) for dev in range(4)]))
+    piece_rows = jnp.roll(
+        jnp.concatenate(ring[::-1], axis=0), (lax.axis_index("tp") + 1) * ring[0].shape[0], axis=0
+    )
     piece_docs = lax.all_gather(doc_rows, "tp", axis=0, tiled=True)
     piece_count = piece_rows.shape[0]
     positions = jnp.arange(piece_count, dtype=jnp.int32)

time: 93.1 us -> 85 us (0.913)
  between operations: 15 us -> 1.75 us
  local copies, waits for them, and re-layouts: 4.37 us -> 14.5 us
  waiting for transfers between devices: 45.4 us -> 36.8 us
  blocking collectives: 8.44 us -> 11.3 us
  matrix products: 12.9 us -> 10.6 us
  starting transfers between devices: 1.92 us -> 3.55 us
  other arithmetic: 4.79 us -> 5.98 us
    all_gather x1 -> x0, waiting for transfers between devices: 35.9 us -> none  [per_device(): piece_rows = lax.all_gather(picked, 'tp', axis=0, tiled=True)]
    ppermute x0 -> x3, waiting for transfers between devices: none -> 27.4 us  [per_device(): lax.ppermute(ring[-1], 'tp', [(dev, (dev + 1) % 4) for dev in range(4)])]
    unnamed x15 -> x32, local copies, waits for them, and re-layouts: 1.67 us -> 11.8 us
    dot_general x3, matrix products: 10.4 us -> 6.45 us  [project(): product = jnp.dot(normed, weight, preferred_element_type=jnp.float32)]
    all_gather x1, blocking collectives: 8.44 us -> 11.3 us  [per_device(): piece_docs = lax.all_gather(doc_rows, 'tp', axis=0, tiled=True)]
    dynamic_slice x1 -> x0, local copies, waits for them, and re-layouts: 1.87 us -> none  [per_device(): picked = lax.dynamic_index_in_dim(stash[0], chosen_slot, 0, keepdims=False)]
    reduce_sum x1, other arithmetic: 2.23 us -> 0.5 us  [normalize(): mean_square = jnp.mean(widened * widened, axis=-1, keepdims=True)]
    ppermute x0 -> x3, starting transfers between devices: none -> 1.63 us  [per_device(): lax.ppermute(ring[-1], 'tp', [(dev, (dev + 1) % 4) for dev in range(4)])]
  transfers between devices with their start and end apart: 2 -> 4, of which waited for: 2 -> 3; matrix products, arithmetic and copies ran while one was open for 2% -> 10% of each run, Pallas kernels for 0% -> 0%
where the time goes in v1:
time: 85 us; the launch traced here: 84.5 us
  waiting for transfers between devices  36.8 us (43%)
  local copies, waits for them, and re-layouts  14.5 us (17%)
  blocking collectives  11.3 us (13%)
  matrix products  10.6 us (12%)
  other arithmetic  5.98 us (7%)
  starting transfers between devices  3.55 us (4%)
  between operations  1.75 us (2%)
    ppermute x3, waiting for transfers between devices, per_device(): lax.ppermute(ring[-1], 'tp', [(dev, (dev + 1) % 4) for dev in range(4)])  27.4 us
    unnamed x32, local copies, waits for them, and re-layouts  11.8 us
    all_gather x1, blocking collectives, per_device(): piece_docs = lax.all_gather(doc_rows, 'tp', axis=0, tiled=True)  11.3 us
    ppermute x1, waiting for transfers between devices, from_behind(): return lax.ppermute(block, axis, route)  9.47 us
    dot_general x3, matrix products, project(): product = jnp.dot(normed, weight, preferred_element_type=jnp.float32)  6.45 us
    sub x1, matrix products, attend(): score_exponent = jnp.exp(scores - row_max)  2.24 us
    ppermute x1, starting transfers between devices, from_behind(): return lax.ppermute(block, axis, route)  1.92 us
    dot_general x1, matrix products, attend(): jnp.einsum('hgij,jhd->ihgd', softmax_weights, value_heads, preferred_elem...  1.91 us
  transfers between devices with their start and end apart: 4, of which 3 were waited for; matrix products, arithmetic and copies ran while one was open for 10% of the time, Pallas kernels for 0%

profile of v1, /device:TPU:4, one launch (start us, length us, event | category | flops | bytes accessed | tf_op | source)
XLA Modules:
  0.0 84.5 jit_solution(6653867898233670130)
XLA Ops:
  0.0 0.0 copy-start
  0.0 0.0 copy-start.1
  0.8 1.1 %dynamic-slice_bitcast_fusion = bf16[64,4096]{1,0:T(8,128)(2,1)S(1)} fusion(bf16[1,2,64,4096]{3,2,1,0:T(8,128)(2,1)} %param.7, s32[]{:T(128)S(6)} %select_n.23), kind=kLoop, calls=%fused_computation.22 | loop fusion | bytes 1048580 | tf_op jit(solution)/shard_map/jit(dynamic_index_in_dim)/squeeze | solution.py:76
  2.0 1.6 %collective-permute-start = (bf16[64,4096]{1,0:T(8,128)(2,1)S(1)}, bf16[64,4096]{1,0:T(8,128)(2,1)}, u32[]{:S(2)}, u32[]{:S(2)}) collective-permute-start(bf16[64,4096]{1,0:T(8,128)(2,1)S(1)} %dynamic-slice_bitcast_fusion), channel_id=1, source_target_pairs={{0,1},{1,2},{2,3},{3,0},{4,5},{5,6},{6,7},{7,4},{8,9},{9,10},{10,1... | collective-permute-start | bytes 1572872 | tf_op jit(solution)/shard_map/ppermute | solution.py:81
  3.6 14.1 %collective-permute-done = bf16[64,4096]{1,0:T(8,128)(2,1)} collective-permute-done((bf16[64,4096]{1,0:T(8,128)(2,1)S(1)}, bf16[64,4096]{1,0:T(8,128)(2,1)}, u32[]{:S(2)}, u32[]{:S(2)}) %collective-permute-start) | collective-permute-done | bytes 524320 | tf_op jit(solution)/shard_map/ppermute | solution.py:81
  17.6 0.0 collective-permute-start.1
  17.6 0.7 convert_element_type.52
  18.4 0.9 %multiply_cosine_fusion = (f32[256,64]{0,1:T(8,128)}, f32[256,64]{0,1:T(8,128)S(1)}) fusion(f32[64]{0:T(128)S(1)} %multiply_power_fusion, f32[256]{0:T(256)S(1)} %iota_convert_fusion), kind=kLoop, calls=%fused_computation.33 | loop fusion | flops 16384 | bytes 132352 | tf_op jit(solution)/shard_map/cos | solution.py:24
  19.3 13.3 %collective-permute-done.1 = bf16[64,4096]{1,0:T(8,128)(2,1)} collective-permute-done((bf16[64,4096]{1,0:T(8,128)(2,1)}, bf16[64,4096]{1,0:T(8,128)(2,1)}, u32[]{:S(2)}, u32[]{:S(2)}) %collective-permute-start.1) | collective-permute-done | bytes 524320 | tf_op jit(solution)/shard_map/ppermute | solution.py:81
  32.6 0.0 collective-permute-start.2
  32.6 0.1 copy.9
  32.7 0.9 %pad_maximum_fusion = f32[256,128]{0,1:T(8,128)S(1)} fusion(f32[256,64]{0,1:T(8,128)} %get-tuple-element.9), kind=kLoop, calls=%fused_computation.30 | loop fusion | flops 32768 | bytes 196608 | tf_op jit(solution)/shard_map/concatenate | solution.py:24
  33.7 0.8 copy.8
  34.4 1.3 %dynamic-slice.2 = u32[1]{0:T(128)} dynamic-slice(u32[32]{0:T(128)} %constant.66, u32[]{:T(128)S(6)} %add.46), dynamic_slice_sizes={1} | dynamic-slice | bytes 12
  36.3 0.6 broadcast.42
  36.9 1.3 %fusion.18 = s32[256]{0:T(256)} fusion(s32[256]{0:T(256)} %broadcast.42, u32[]{:T(128)} %bitcast.6, s32[1,2,64]{2,1,0:T(2,128)} %param.9, s32[]{:T(128)S(6)} %select_n.23), kind=kLoop, calls=%fused_computation.46 | loop fusion | bytes 1540
  38.2 11.3 %all-reduce = s32[256]{0:T(256)} all-reduce(s32[256]{0:T(256)} %fusion.18), channel_id=2, replica_groups=mesh['section'=8,'tp'=4] {'tp'}, use_global_device_ids=true, to_apply=%add | all-reduce | flops 256 | bytes 2048 | tf_op jit(solution)/shard_map/all_gather | solution.py:85
  49.5 1.5 %fusion.12 = pred[256,256]{0,1:T(8,128)(4,1)} fusion(s32[256]{0:T(256)} %all-reduce), kind=kLoop, calls=%fused_computation.28 | loop fusion | flops 196608 | bytes 66560 | tf_op jit(solution)/shard_map/and | solution.py:58
  51.0 0.0 collective-permute-done.2
  51.0 1.1 %constant_dynamic-update-slice_fusion.7 = bf16[512,4096]{1,0:T(8,128)(2,1)S(1)} fusion(bf16[64,4096]{1,0:T(8,128)(2,1)} %collective-permute-done.2), kind=kLoop, calls=%fused_computation.41 | loop fusion | bytes 1048576
  52.1 1.1 %constant_dynamic-update-slice_fusion.6 = bf16[512,4096]{1,0:T(8,128)(2,1)S(1)} fusion(bf16[512,4096]{1,0:T(8,128)(2,1)S(1)} %constant_dynamic-update-slice_fusion.7, bf16[64,4096]{1,0:T(8,128)(2,1)} %collective-permute-done.1), kind=kLoop, calls=%fused_computation.40 | loop fusion | bytes 1048576
  53.1 0.0 copy-start.8
  53.2 1.2 %constant_dynamic-update-slice_fusion.5 = bf16[512,4096]{1,0:T(8,128)(2,1)S(1)} fusion(bf16[512,4096]{1,0:T(8,128)(2,1)S(1)} %constant_dynamic-update-slice_fusion.6, bf16[64,4096]{1,0:T(8,128)(2,1)} %collective-permute-done), kind=kLoop, calls=%fused_computation.39 | loop fusion | bytes 1048576
  54.4 0.0 copy-done.1
  54.4 1.3 %constant_dynamic-update-slice_fusion.3 = bf16[512,4096]{1,0:T(8,128)(2,1)S(1)} fusion(bf16[512,4096]{1,0:T(8,128)(2,1)S(1)} %constant_dynamic-update-slice_fusion.4, bf16[64,4096]{1,0:T(8,128)(2,1)} %collective-permute-done.2), kind=kLoop, calls=%fused_computation.37 | loop fusion | bytes 1048576
  55.8 1.1 %constant_dynamic-update-slice_fusion.2 = bf16[512,4096]{1,0:T(8,128)(2,1)S(1)} fusion(bf16[512,4096]{1,0:T(8,128)(2,1)S(1)} %constant_dynamic-update-slice_fusion.3, bf16[64,4096]{1,0:T(8,128)(2,1)} %collective-permute-done.1), kind=kLoop, calls=%fused_computation.36 | loop fusion | bytes 1048576
  56.9 1.1 %constant_dynamic-update-slice_fusion.1 = bf16[512,4096]{1,0:T(8,128)(2,1)S(1)} fusion(bf16[512,4096]{1,0:T(8,128)(2,1)S(1)} %constant_dynamic-update-slice_fusion.2, bf16[64,4096]{1,0:T(8,128)(2,1)} %collective-permute-done), kind=kLoop, calls=%fused_computation.35 | loop fusion | bytes 1048576
  58.1 0.0 copy-start.2
  58.1 0.5 fusion.1
  58.6 0.0 copy-done.8
  58.6 0.0 copy-start.6
  58.6 2.4 %fusion.23 = f32[256,1024]{1,0:T(8,128)S(1)} fusion(bf16[4096,1024]{1,0:T(8,128)(2,1)S(1)} %copy-done.8, f32[4096]{0:T(1024)S(1)} %convert_element_type.52, f32[256]{0:T(256)S(1)} %add_rsqrt_fusion, bf16[512,4096]{1,0:T(8,128)(2,1)S(1)} %constant_dynamic-update-slice_fusion, s32[]{:T(128)S(6)} %select_n.25), kind=kOutput, calls=%fused_computation.50 | convolution fusion | flops 2151677952 | bytes 11551748 | tf_op jit(solution)/shard_map/dot_general | solution.py:40
  61.0 0.0 copy-done.2
  61.0 0.0 copy-done.6
  61.0 0.2 copy.20
  61.2 0.0 copy-start.4
  61.2 0.3 slice_negate_fusion
  61.6 0.4 maximum_multiply_fusion
  61.9 0.0 copy-start.7
  61.9 0.2 copy-done.4
  62.1 0.1 mul.133
  62.2 0.6 fusion.5
  62.8 0.4 reshape.69
  63.2 0.0 copy-done
  63.2 0.0 copy-done.7
  63.2 0.0 copy-start.3
  63.2 0.0 copy-start.9
  63.2 2.9 %fusion.25 = f32[256,256]{0,1:T(8,128)S(1)} fusion(bf16[4096,256]{1,0:T(8,128)(2,1)S(1)} %copy-done, f32[4096]{0:T(1024)S(1)} %convert_element_type.52, f32[256]{0:T(256)S(1)} %copy-done.7, bf16[512,4096]{1,0:T(8,128)(2,1)} %copy-done.2, s32[]{:T(128)S(6)} %select_n.25), kind=kOutput, calls=%fused_computation.51 | convolution fusion | flops 541065216 | bytes 4473860 | tf_op jit(solution)/shard_map/dot_general | solution.py:40
  66.1 0.0 copy-start.5
  66.2 0.0 copy-done.3
  66.2 0.5 copy-done.9
  66.7 1.2 %convolution_convert_fusion.1 = bf16[256,256]{0,1:T(8,128)(2,1)S(1)} fusion(bf16[4096,256]{1,0:T(8,128)(2,1)S(1)} %copy-done.9, f32[4096]{0:T(1024)S(1)} %convert_element_type.52, f32[256]{0:T(256)S(1)} %copy-done.7, bf16[512,4096]{1,0:T(8,128)(2,1)S(1)} %copy-done.3, s32[]{:T(128)S(6)} %select_n.25), kind=kOutput, calls=%fused_computation.11 | convolution fusion | flops 541130752 | bytes 4342788 | tf_op jit(solution)/shard_map/dot_general | solution.py:40
  67.9 0.0 copy-done.5
  67.9 2.2 %fusion.28 = (f32[2,4,256]{2,1,0:T(4,128)S(1)}, f32[2,4,256,256]{2,3,1,0:T(8,128)}) fusion(pred[256,256]{0,1:T(8,128)(4,1)S(1)} %copy-done.5, bf16[256,2,128,1]{0,2,3,1:T(8,128)(2,1)S(1)} %bitcast.67, bf16[256,2,4,128]{3,2,1,0:T(4,128)(2,1)S(1)} %reshape.69), kind=kOutput, calls=%fused_computation.52 | convolution fusion | flops 136315136 | bytes 2826240 | tf_op jit(solution)/shard_map/sub | solution.py:61
  70.1 1.9 %convolution_convert_fusion = bf16[2,128,4,256]{3,1,2,0:T(8,128)(2,1)S(1)} fusion(bf16[256,2,128,1]{0,2,3,1:T(8,128)(2,1)S(1)} %bitcast.68, f32[2,4,256,256]{2,3,1,0:T(8,128)} %get-tuple-element.12, f32[2,4,256]{2,1,0:T(4,128)S(1)} %get-tuple-element.11), kind=kOutput, calls=%fused_computation.10 | convolution fusion | flops 135528448 | bytes 2760704 | tf_op jit(solution)/shard_map/hgij,jhd->ihgd/dot_general | solution.py:65
  72.1 0.2 copy.13
  72.3 1.9 %collective-permute-start.3 = (bf16[1,256,1024]{2,1,0:T(8,128)(2,1)S(1)}, bf16[1,256,1024]{2,1,0:T(8,128)(2,1)S(1)}, u32[]{:S(2)}, u32[]{:S(2)}) collective-permute-start(bf16[1,256,1024]{2,1,0:T(8,128)(2,1)S(1)} %copy.13), channel_id=1, source_target_pairs={{0,4},{4,8},{8,12},{12,16},{16,20},{20,24},{24,28},{1,5},{5,9},{9,... | collective-permute-start | bytes 1572872 | tf_op jit(solution)/shard_map/ppermute | solution.py:15
  74.2 9.5 %collective-permute-done.3 = bf16[1,256,1024]{2,1,0:T(8,128)(2,1)S(1)} collective-permute-done((bf16[1,256,1024]{2,1,0:T(8,128)(2,1)S(1)}, bf16[1,256,1024]{2,1,0:T(8,128)(2,1)S(1)}, u32[]{:S(2)}, u32[]{:S(2)}) %collective-permute-start.3) | collective-permute-done | bytes 524320 | tf_op jit(solution)/shard_map/ppermute | solution.py:15
  83.7 0.8 copy.44
  (9 shorter events, 0.2 us)
Async XLA Ops:
  0.0 63.2 %copy-start = (bf16[4096,256]{1,0:T(8,128)(2,1)S(1)}, bf16[4096,256]{1,0:T(8,128)(2,1)}, u32[]{:S(2)}) copy-start(bf16[4096,256]{1,0:T(8,128)(2,1)} %param.12) | copy-start | bytes 6291460
  0.0 54.4 %copy-start.1 = (bf16[1,2,64,4096]{3,2,1,0:T(8,128)(2,1)S(1)}, bf16[1,2,64,4096]{3,2,1,0:T(8,128)(2,1)}, u32[]{:S(2)}) copy-start(bf16[1,2,64,4096]{3,2,1,0:T(8,128)(2,1)} %param.7) | copy-start | bytes 3145732
  2.0 15.7 %collective-permute-start = (bf16[64,4096]{1,0:T(8,128)(2,1)S(1)}, bf16[64,4096]{1,0:T(8,128)(2,1)}, u32[]{:S(2)}, u32[]{:S(2)}) collective-permute-start(bf16[64,4096]{1,0:T(8,128)(2,1)S(1)} %dynamic-slice_bitcast_fusion), channel_id=1, source_target_pairs={{0,1},{1,2},{2,3},{3,0},{4,5},{5,6},{6,7},{7,4},{8,9},{9,10},{10,1... | collective-permute-start | bytes 1572872 | tf_op jit(solution)/shard_map/ppermute | solution.py:81
  17.6 15.0 %collective-permute-start.1 = (bf16[64,4096]{1,0:T(8,128)(2,1)}, bf16[64,4096]{1,0:T(8,128)(2,1)}, u32[]{:S(2)}, u32[]{:S(2)}) collective-permute-start(bf16[64,4096]{1,0:T(8,128)(2,1)} %collective-permute-done), channel_id=1, source_target_pairs={{0,1},{1,2},{2,3},{3,0},{4,5},{5,6},{6,7},{7,4},{8,9},{9,10},{10,1... | collective-permute-start | bytes 1572872 | tf_op jit(solution)/shard_map/ppermute | solution.py:81
  32.6 18.4 %collective-permute-start.2 = (bf16[64,4096]{1,0:T(8,128)(2,1)}, bf16[64,4096]{1,0:T(8,128)(2,1)}, u32[]{:S(2)}, u32[]{:S(2)}) collective-permute-start(bf16[64,4096]{1,0:T(8,128)(2,1)} %collective-permute-done.1), channel_id=1, source_target_pairs={{0,1},{1,2},{2,3},{3,0},{4,5},{5,6},{6,7},{7,4},{8,9},{9,10},{10,1... | collective-permute-start | bytes 1572872 | tf_op jit(solution)/shard_map/ppermute | solution.py:81
  53.1 5.4 %copy-start.8 = (bf16[4096,1024]{1,0:T(8,128)(2,1)S(1)}, bf16[4096,1024]{1,0:T(8,128)(2,1)}, u32[]{:S(2)}) copy-start(bf16[4096,1024]{1,0:T(8,128)(2,1)} %param.11) | copy-start | bytes 25165828
  58.1 2.9 %copy-start.2 = (bf16[512,4096]{1,0:T(8,128)(2,1)}, bf16[512,4096]{1,0:T(8,128)(2,1)S(1)}, u32[]{:S(2)}) copy-start(bf16[512,4096]{1,0:T(8,128)(2,1)S(1)} %constant_dynamic-update-slice_fusion) | copy-start | bytes 12582916
  58.6 2.4 %copy-start.6 = (f32[256]{0:T(256)}, f32[256]{0:T(256)S(1)}, u32[]{:S(2)}) copy-start(f32[256]{0:T(256)S(1)} %add_rsqrt_fusion) | copy-start | bytes 3076
  61.2 0.9 %copy-start.4 = (f32[256,128]{1,0:T(8,128)S(1)}, f32[256,128]{1,0:T(8,128)}, u32[]{:S(2)}) copy-start(f32[256,128]{1,0:T(8,128)} %copy.8) | copy-start | bytes 393220
  61.9 1.2 %copy-start.7 = (f32[256]{0:T(256)S(1)}, f32[256]{0:T(256)}, u32[]{:S(2)}) copy-start(f32[256]{0:T(256)} %copy-done.6) | copy-start | bytes 3076
  63.2 3.0 %copy-start.3 = (bf16[512,4096]{1,0:T(8,128)(2,1)S(1)}, bf16[512,4096]{1,0:T(8,128)(2,1)}, u32[]{:S(2)}) copy-start(bf16[512,4096]{1,0:T(8,128)(2,1)} %copy-done.2) | copy-start | bytes 12582916
  63.2 3.5 %copy-start.9 = (bf16[4096,256]{1,0:T(8,128)(2,1)S(1)}, bf16[4096,256]{1,0:T(8,128)(2,1)}, u32[]{:S(2)}) copy-start(bf16[4096,256]{1,0:T(8,128)(2,1)} %param.13) | copy-start | bytes 6291460
  66.1 1.8 %copy-start.5 = (pred[256,256]{0,1:T(8,128)(4,1)S(1)}, pred[256,256]{0,1:T(8,128)(4,1)}, u32[]{:S(2)}) copy-start(pred[256,256]{0,1:T(8,128)(4,1)} %fusion.12) | copy-start | bytes 196612
  72.3 11.4 %collective-permute-start.3 = (bf16[1,256,1024]{2,1,0:T(8,128)(2,1)S(1)}, bf16[1,256,1024]{2,1,0:T(8,128)(2,1)S(1)}, u32[]{:S(2)}, u32[]{:S(2)}) collective-permute-start(bf16[1,256,1024]{2,1,0:T(8,128)(2,1)S(1)} %copy.13), channel_id=1, source_target_pairs={{0,4},{4,8},{8,12},{12,16},{16,20},{20,24},{24,28},{1,5},{5,9},{9,... | collective-permute-start | bytes 1572872 | tf_op jit(solution)/shard_map/ppermute | solution.py:15
